TPU v7x, 32 devices: a 4x4x1 block of a 4x4x8 slice. The times are simulated.
32 devices in a mesh: data: 1 (over z), inner: 4 (over y), stage: 8 (over x, core).
Axes of the slice: x: 4, y: 4, z: 1, core: 2. Of those that a mesh axis runs over, the one named last changes fastest.
The devices are a block of a 4x4x8 slice.
Arguments:
- x: bfloat16 [8, 256, 1024], P(('data', 'stage'), 'inner')
- g: bfloat16 [8, 256, 1024], P(('data', 'stage'), 'inner')
- w1: bfloat16 [1, 8, 1024, 4096], P(None, 'stage')
- w2: bfloat16 [1, 8, 4096, 1024], P(None, 'stage')
Outputs:
- output 1: bfloat16 [8, 256, 1024], P(('data', 'stage'), 'inner')
- output 2: bfloat16 [8, 256, 1024], P(('data', 'stage'), 'inner')
- output 3: float32 [1, 8, 1024, 4096], P('data', 'stage')
- output 4: float32 [1, 8, 4096, 1024], P('data', 'stage')
All inputs are finite; a program needn't handle non-finite values.
Results may differ from a plain program's by a relative error of at most 0.02.
Values are sent between devices in bfloat16 or wider.
A program may use at most 768 MiB of HBM per device.

v0:
```python
import jax
import jax.numpy as jnp
from jax import lax
from jax.sharding import PartitionSpec as P


def _gelu(t):
    return jax.nn.gelu(t, approximate=True)


def _fwd(h, w1, w2):
    z = jnp.dot(h, w1, preferred_element_type=jnp.float32)
    a = _gelu(z).astype(jnp.bfloat16)
    u = jnp.dot(a, w2, preferred_element_type=jnp.float32)
    return (h.astype(jnp.float32) + u).astype(jnp.bfloat16)


def _bwd(h, dh, w1, w2):
    z = jnp.dot(h, w1, preferred_element_type=jnp.float32)
    a32, gelu_vjp = jax.vjp(_gelu, z)
    a = a32.astype(jnp.bfloat16)
    dw2 = jnp.dot(a.T, dh, preferred_element_type=jnp.float32)
    da = jnp.dot(dh, w2.T, preferred_element_type=jnp.float32)
    dz = gelu_vjp(da)[0].astype(jnp.bfloat16)
    dw1 = jnp.dot(h.T, dz, preferred_element_type=jnp.float32)
    dh_prev = (dh.astype(jnp.float32) + jnp.dot(dz, w1.T, preferred_element_type=jnp.float32)).astype(jnp.bfloat16)
    return dh_prev, dw1, dw2


def solution(mesh):
    n_stage = mesh.shape["stage"]
    fwd_perm = [(i, (i + 1) % n_stage) for i in range(n_stage)]
    bwd_perm = [(i, (i - 1) % n_stage) for i in range(n_stage)]

    def body(x, g, w1, w2):
        p = lax.axis_index("stage")
        q = n_stage - 1 - p
        nv, k, d, f = w1.shape
        mb, bl, _ = x.shape
        m = mb * n_stage
        n_ticks = nv * m + n_stage - 1
        x_all = lax.all_gather(x, "stage", axis=0, tiled=True)
        g_all = lax.all_gather(g, "stage", axis=0, tiled=True)

        def slot(s):
            valid = (s >= 0) & (s < nv * m)
            sc = jnp.clip(s, 0, nv * m - 1)
            return valid, sc // m, sc % m

        def fwd_tick(carry, t):
            inc, buf, saved, y_all = carry
            ok_in, _, m_in = slot(t - n_stage)
            buf = buf.at[m_in].set(jnp.where(ok_in & (p == 0), inc, buf[m_in]))
            ok, v, mi = slot(t - p)
            h = jnp.where(p == 0, jnp.where(v == 0, x_all[mi], buf[mi]), inc)
            w1v, w2v = w1[v], w2[v]
            hs = []
            for j in range(k):
                hs.append(h)
                h = _fwd(h, w1v[j], w2v[j])
            saved = saved.at[v, mi].set(jnp.where(ok, jnp.stack(hs), saved[v, mi]))
            last = ok & (p == n_stage - 1) & (v == nv - 1)
            y_all = y_all.at[mi].set(jnp.where(last, h, y_all[mi]))
            inc = lax.ppermute(h, "stage", fwd_perm)
            return (inc, buf, saved, y_all), None

        act0 = jnp.zeros((bl, d), jnp.bfloat16)
        per_mb0 = jnp.zeros((m, bl, d), jnp.bfloat16)
        saved0 = jnp.zeros((nv, m, k, bl, d), jnp.bfloat16)
        ticks = jnp.arange(n_ticks, dtype=jnp.int32)
        (_, _, saved, y_all), _ = lax.scan(fwd_tick, (act0, per_mb0, saved0, per_mb0), ticks)

        def bwd_tick(carry, t):
            inc, buf, dw1, dw2, dx_all = carry
            ok_in, _, m_in = slot(t - n_stage)
            buf = buf.at[m_in].set(jnp.where(ok_in & (q == 0), inc, buf[m_in]))
            ok, u, mi = slot(t - q)
            v = nv - 1 - u
            dh = jnp.where(q == 0, jnp.where(u == 0, g_all[mi], buf[mi]), inc)
            hs = saved[v, mi]
            w1v, w2v = w1[v], w2[v]
            d1s = [None] * k
            d2s = [None] * k
            for j in reversed(range(k)):
                dh, d1s[j], d2s[j] = _bwd(hs[j], dh, w1v[j], w2v[j])
            on = ok.astype(jnp.float32)
            dw1 = dw1.at[v].add(jnp.stack(d1s) * on)
            dw2 = dw2.at[v].add(jnp.stack(d2s) * on)
            first = ok & (p == 0) & (v == 0)
            dx_all = dx_all.at[mi].set(jnp.where(first, dh, dx_all[mi]))
            inc = lax.ppermute(dh, "stage", bwd_perm)
            return (inc, buf, dw1, dw2, dx_all), None

        dw1_0 = jnp.zeros((nv, k, d, f), jnp.float32)
        dw2_0 = jnp.zeros((nv, k, f, d), jnp.float32)
        (_, _, dw1, dw2, dx_all), _ = lax.scan(bwd_tick, (act0, per_mb0, dw1_0, dw2_0, per_mb0), ticks)

        zero = jnp.zeros_like(y_all)
        y = lax.psum_scatter(jnp.where(p == n_stage - 1, y_all, zero), "stage", scatter_dimension=0, tiled=True)
        dx = lax.psum_scatter(jnp.where(p == 0, dx_all, zero), "stage", scatter_dimension=0, tiled=True)
        dw1 = lax.psum(dw1, "inner")
        dw2 = lax.psum(dw2, "inner")
        return y, dx, dw1, dw2

    tok = P(("data", "stage"), "inner", None)
    wsp = P(None, "stage", None, None)
    dsp = P("data", "stage", None, None)
    return jax.shard_map(body, mesh=mesh, in_specs=(tok, tok, wsp, wsp), out_specs=(tok, tok, dsp, dsp), check_vma=False)
```

profile of v0, /device:TPU:96, one launch (start us, length us, event | category | flops | bytes accessed | tf_op | source)
XLA Modules:
  0.0 1676.5 jit_solution(2131705177585606931)
XLA Ops:
  8.9 23.9 %all-gather.3.cloned.1.call-done = bf16[8,64,1024]{2,1,0:T(8,128)(2,1)} async-done(((bf16[1,64,1024]{2,1,0:T(8,128)(2,1)}), bf16[8,64,1024]{2,1,0:T(8,128)(2,1)}) %all-gather.3.cloned.1.call-update) | async-done | bytes 1048592 | tf_op jit(solution)/shard_map/all_gather | solution.py:42
  34.1 363.8 %while.46 = (s32[]{:T(128)}, bf16[64,1024]{1,0:T(8,128)(2,1)S(1)}, bf16[8,64,1024]{2,1,0:T(8,128)(2,1)}, bf16[1,8,1,64,1024]{4,3,2,1,0:T(8,128)(2,1)S(1)}, bf16[...) while((s32[]{:T(128)}, bf16[64,1024]{1,0:T(8,128)(2,1)S(1)}, ...), condition=%wide.region_4.5_spmd, body=%wide.region_0.4_spmd.sunk | while | flops 1076822144 | bytes 19925264 | solution.py:71
  43.0 9.7 fusion.100
  67.3 9.7 fusion.100
  91.5 9.7 fusion.100
  115.8 9.7 fusion.100
  140.0 9.7 fusion.100
  164.3 9.7 fusion.100
  188.5 9.7 fusion.100
  212.8 9.7 fusion.100
  261.3 9.7 fusion.100
  285.5 9.7 fusion.100
  309.8 9.7 fusion.100
  334.1 9.7 fusion.100
  358.3 9.7 fusion.100
  382.6 9.7 fusion.100
  400.6 650.9 %while.47 = (s32[]{:T(128)}, bf16[64,1024]{1,0:T(8,128)(2,1)S(1)}, bf16[8,64,1024]{2,1,0:T(8,128)(2,1)S(1)}, f32[1,1,1024,4096]{3,2,1,0:T(8,128)}, f32[1,1,4096,...) while((s32[]{:T(128)}, bf16[64,1024]{1,0:T(8,128)(2,1)S(1)}, ...), condition=%wide.region_10.11_spmd.clone, body=%wide.region_6.10_spmd.clone.sunk | while | flops 2726100992 | bytes 167120272 | solution.py:96
  457.6 11.7 add_select_fusion.5
  469.3 11.6 add_select_fusion.4
  501.1 11.7 add_select_fusion.5
  512.8 11.6 add_select_fusion.4
  544.5 11.7 add_select_fusion.5
  556.2 11.6 add_select_fusion.4
  588.0 11.7 add_select_fusion.5
  599.7 11.6 add_select_fusion.4
  631.5 11.7 add_select_fusion.5
  643.2 11.6 add_select_fusion.4
  675.4 11.7 add_select_fusion.5
  687.1 11.6 add_select_fusion.4
  723.5 11.7 add_select_fusion.5
  735.2 11.6 add_select_fusion.4
  767.0 11.7 add_select_fusion.5
  778.7 11.6 add_select_fusion.4
  810.5 11.7 add_select_fusion.5
  822.2 11.6 add_select_fusion.4
  854.0 11.7 add_select_fusion.5
  865.7 11.6 add_select_fusion.4
  897.5 11.7 add_select_fusion.5
  909.2 11.6 add_select_fusion.4
  940.9 11.7 add_select_fusion.5
  952.6 11.6 add_select_fusion.4
  984.4 11.7 add_select_fusion.5
  996.1 11.6 add_select_fusion.4
  1028.2 11.7 add_select_fusion.5
  1039.9 11.6 add_select_fusion.4
  1054.6 30.9 %reduce-scatter.5.cloned.1.call-done = bf16[1,64,1024]{2,1,0:T(8,128)(2,1)} async-done(((bf16[8,64,1024]{2,1,0:T(8,128)(2,1)}), bf16[1,64,1024]{2,1,0:T(8,128)(2,1)}) %reduce-scatter.5.cloned.1.call-update) | async-done | bytes 131088 | tf_op jit(solution)/shard_map/reduce_scatter | solution.py:100
  1085.4 561.9 %all-reduce.3.cloned.1.call-done = (f32[1,1,1024,4096]{3,2,1,0:T(8,128)}, f32[1,1,4096,1024]{3,2,1,0:T(8,128)}) async-done(((f32[1,1,1024,4096]{3,2,1,0:T(8,128)}, f32[1,1,4096,1024]{3,2,1,0:T(8,128)}), (f32[1,1,1024,4096]{3,2,1,0:T(8,128)}, f32[1,1,4096,1024]{3,2,1,0:T(8,128)})) %all-reduce.3.cloned.1.call-update) | async-done | bytes 33554448 | tf_op jit(solution)/shard_map/psum | solution.py:101
  1647.4 12.6 copy.48
  (511 shorter events, 529.6 us)
Async XLA Ops:
  7.2 25.6 %all-gather.3.cloned.1.call-start = ((), (), s32[]{:S(2)}) async-start(), calls=%async_computation.2 | async-start | bytes 1179648 | tf_op jit(solution)/shard_map/all_gather | solution.py:42
  8.0 391.4 %all-gather.5.cloned.1.call-start = ((), (), s32[]{:S(2)}) async-start(), calls=%async_computation.4 | async-start | bytes 1179648 | tf_op jit(solution)/shard_map/all_gather | solution.py:43
  8.8 1045.8 %reduce-scatter.3.cloned.1.call-start = ((), (), s32[]{:S(2)}) async-start(), calls=%async_computation.3 | async-start | bytes 1179648 | tf_op jit(solution)/shard_map/reduce_scatter | solution.py:99
  52.8 5.6 collective-permute-start
  77.0 5.6 collective-permute-start
  101.3 5.6 collective-permute-start
  125.5 5.6 collective-permute-start
  149.8 5.6 collective-permute-start
  174.0 5.6 collective-permute-start
  198.3 5.6 collective-permute-start
  222.5 5.6 collective-permute-start
  246.8 5.6 collective-permute-start
  271.0 5.6 collective-permute-start
  295.3 5.6 collective-permute-start
  319.5 5.6 collective-permute-start
  343.8 5.6 collective-permute-start
  368.0 5.6 collective-permute-start
  392.3 5.6 collective-permute-start
  399.1 686.4 %reduce-scatter.5.cloned.1.call-start = ((), (), s32[]{:S(2)}) async-start(), calls=%async_computation.5 | async-start | bytes 1179648 | tf_op jit(solution)/shard_map/reduce_scatter | solution.py:100
  402.7 13.4 slice-start
  420.0 17.4 %collective-permute-start.1 = (bf16[64,1024]{1,0:T(8,128)(2,1)S(1)}, bf16[64,1024]{1,0:T(8,128)(2,1)S(1)}, u32[]{:S(2)}, u32[]{:S(2)}) collective-permute-start(bf16[64,1024]{1,0:T(8,128)(2,1)S(1)} %get-tuple-element.707), channel_id=1, source_target_pairs={{0,7},{1,0},{2,1},{3,2},{4,3},{5,4},{6,5},{7,6},{8,15},{9,8},{10,9... | collective-permute-start | bytes 393224 | tf_op jit(solution)/shard_map/while/body/eval_jaxpr/ppermute | solution.py:91
  439.4 13.4 slice-start
  456.8 24.1 %collective-permute-start.1 = (bf16[64,1024]{1,0:T(8,128)(2,1)S(1)}, bf16[64,1024]{1,0:T(8,128)(2,1)S(1)}, u32[]{:S(2)}, u32[]{:S(2)}) collective-permute-start(bf16[64,1024]{1,0:T(8,128)(2,1)S(1)} %get-tuple-element.707), channel_id=1, source_target_pairs={{0,7},{1,0},{2,1},{3,2},{4,3},{5,4},{6,5},{7,6},{8,15},{9,8},{10,9... | collective-permute-start | bytes 393224 | tf_op jit(solution)/shard_map/while/body/eval_jaxpr/ppermute | solution.py:91
  482.9 13.4 slice-start
  500.3 24.1 %collective-permute-start.1 = (bf16[64,1024]{1,0:T(8,128)(2,1)S(1)}, bf16[64,1024]{1,0:T(8,128)(2,1)S(1)}, u32[]{:S(2)}, u32[]{:S(2)}) collective-permute-start(bf16[64,1024]{1,0:T(8,128)(2,1)S(1)} %get-tuple-element.707), channel_id=1, source_target_pairs={{0,7},{1,0},{2,1},{3,2},{4,3},{5,4},{6,5},{7,6},{8,15},{9,8},{10,9... | collective-permute-start | bytes 393224 | tf_op jit(solution)/shard_map/while/body/eval_jaxpr/ppermute | solution.py:91
  526.4 13.4 slice-start
  543.8 24.1 %collective-permute-start.1 = (bf16[64,1024]{1,0:T(8,128)(2,1)S(1)}, bf16[64,1024]{1,0:T(8,128)(2,1)S(1)}, u32[]{:S(2)}, u32[]{:S(2)}) collective-permute-start(bf16[64,1024]{1,0:T(8,128)(2,1)S(1)} %get-tuple-element.707), channel_id=1, source_target_pairs={{0,7},{1,0},{2,1},{3,2},{4,3},{5,4},{6,5},{7,6},{8,15},{9,8},{10,9... | collective-permute-start | bytes 393224 | tf_op jit(solution)/shard_map/while/body/eval_jaxpr/ppermute | solution.py:91
  569.9 13.4 slice-start
  587.3 24.1 %collective-permute-start.1 = (bf16[64,1024]{1,0:T(8,128)(2,1)S(1)}, bf16[64,1024]{1,0:T(8,128)(2,1)S(1)}, u32[]{:S(2)}, u32[]{:S(2)}) collective-permute-start(bf16[64,1024]{1,0:T(8,128)(2,1)S(1)} %get-tuple-element.707), channel_id=1, source_target_pairs={{0,7},{1,0},{2,1},{3,2},{4,3},{5,4},{6,5},{7,6},{8,15},{9,8},{10,9... | collective-permute-start | bytes 393224 | tf_op jit(solution)/shard_map/while/body/eval_jaxpr/ppermute | solution.py:91
  613.4 13.4 slice-start
  630.7 24.1 %collective-permute-start.1 = (bf16[64,1024]{1,0:T(8,128)(2,1)S(1)}, bf16[64,1024]{1,0:T(8,128)(2,1)S(1)}, u32[]{:S(2)}, u32[]{:S(2)}) collective-permute-start(bf16[64,1024]{1,0:T(8,128)(2,1)S(1)} %get-tuple-element.707), channel_id=1, source_target_pairs={{0,7},{1,0},{2,1},{3,2},{4,3},{5,4},{6,5},{7,6},{8,15},{9,8},{10,9... | collective-permute-start | bytes 393224 | tf_op jit(solution)/shard_map/while/body/eval_jaxpr/ppermute | solution.py:91
  656.8 13.4 slice-start
  674.2 24.4 %collective-permute-start.1 = (bf16[64,1024]{1,0:T(8,128)(2,1)S(1)}, bf16[64,1024]{1,0:T(8,128)(2,1)S(1)}, u32[]{:S(2)}, u32[]{:S(2)}) collective-permute-start(bf16[64,1024]{1,0:T(8,128)(2,1)S(1)} %get-tuple-element.707), channel_id=1, source_target_pairs={{0,7},{1,0},{2,1},{3,2},{4,3},{5,4},{6,5},{7,6},{8,15},{9,8},{10,9... | collective-permute-start | bytes 393224 | tf_op jit(solution)/shard_map/while/body/eval_jaxpr/ppermute | solution.py:91
  700.7 13.4 slice-start
  718.1 28.7 %collective-permute-start.1 = (bf16[64,1024]{1,0:T(8,128)(2,1)S(1)}, bf16[64,1024]{1,0:T(8,128)(2,1)S(1)}, u32[]{:S(2)}, u32[]{:S(2)}) collective-permute-start(bf16[64,1024]{1,0:T(8,128)(2,1)S(1)} %get-tuple-element.707), channel_id=1, source_target_pairs={{0,7},{1,0},{2,1},{3,2},{4,3},{5,4},{6,5},{7,6},{8,15},{9,8},{10,9... | collective-permute-start | bytes 393224 | tf_op jit(solution)/shard_map/while/body/eval_jaxpr/ppermute | solution.py:91
  748.8 13.4 slice-start
  766.2 24.1 %collective-permute-start.1 = (bf16[64,1024]{1,0:T(8,128)(2,1)S(1)}, bf16[64,1024]{1,0:T(8,128)(2,1)S(1)}, u32[]{:S(2)}, u32[]{:S(2)}) collective-permute-start(bf16[64,1024]{1,0:T(8,128)(2,1)S(1)} %get-tuple-element.707), channel_id=1, source_target_pairs={{0,7},{1,0},{2,1},{3,2},{4,3},{5,4},{6,5},{7,6},{8,15},{9,8},{10,9... | collective-permute-start | bytes 393224 | tf_op jit(solution)/shard_map/while/body/eval_jaxpr/ppermute | solution.py:91
  792.4 13.4 slice-start
  809.8 24.1 %collective-permute-start.1 = (bf16[64,1024]{1,0:T(8,128)(2,1)S(1)}, bf16[64,1024]{1,0:T(8,128)(2,1)S(1)}, u32[]{:S(2)}, u32[]{:S(2)}) collective-permute-start(bf16[64,1024]{1,0:T(8,128)(2,1)S(1)} %get-tuple-element.707), channel_id=1, source_target_pairs={{0,7},{1,0},{2,1},{3,2},{4,3},{5,4},{6,5},{7,6},{8,15},{9,8},{10,9... | collective-permute-start | bytes 393224 | tf_op jit(solution)/shard_map/while/body/eval_jaxpr/ppermute | solution.py:91
  835.8 13.4 slice-start
  853.2 24.1 %collective-permute-start.1 = (bf16[64,1024]{1,0:T(8,128)(2,1)S(1)}, bf16[64,1024]{1,0:T(8,128)(2,1)S(1)}, u32[]{:S(2)}, u32[]{:S(2)}) collective-permute-start(bf16[64,1024]{1,0:T(8,128)(2,1)S(1)} %get-tuple-element.707), channel_id=1, source_target_pairs={{0,7},{1,0},{2,1},{3,2},{4,3},{5,4},{6,5},{7,6},{8,15},{9,8},{10,9... | collective-permute-start | bytes 393224 | tf_op jit(solution)/shard_map/while/body/eval_jaxpr/ppermute | solution.py:91
  896.7 24.1 %collective-permute-start.1 = (bf16[64,1024]{1,0:T(8,128)(2,1)S(1)}, bf16[64,1024]{1,0:T(8,128)(2,1)S(1)}, u32[]{:S(2)}, u32[]{:S(2)}) collective-permute-start(bf16[64,1024]{1,0:T(8,128)(2,1)S(1)} %get-tuple-element.707), channel_id=1, source_target_pairs={{0,7},{1,0},{2,1},{3,2},{4,3},{5,4},{6,5},{7,6},{8,15},{9,8},{10,9... | collective-permute-start | bytes 393224 | tf_op jit(solution)/shard_map/while/body/eval_jaxpr/ppermute | solution.py:91
  922.8 13.4 slice-start
  940.2 24.1 %collective-permute-start.1 = (bf16[64,1024]{1,0:T(8,128)(2,1)S(1)}, bf16[64,1024]{1,0:T(8,128)(2,1)S(1)}, u32[]{:S(2)}, u32[]{:S(2)}) collective-permute-start(bf16[64,1024]{1,0:T(8,128)(2,1)S(1)} %get-tuple-element.707), channel_id=1, source_target_pairs={{0,7},{1,0},{2,1},{3,2},{4,3},{5,4},{6,5},{7,6},{8,15},{9,8},{10,9... | collective-permute-start | bytes 393224 | tf_op jit(solution)/shard_map/while/body/eval_jaxpr/ppermute | solution.py:91
  983.6 24.1 %collective-permute-start.1 = (bf16[64,1024]{1,0:T(8,128)(2,1)S(1)}, bf16[64,1024]{1,0:T(8,128)(2,1)S(1)}, u32[]{:S(2)}, u32[]{:S(2)}) collective-permute-start(bf16[64,1024]{1,0:T(8,128)(2,1)S(1)} %get-tuple-element.707), channel_id=1, source_target_pairs={{0,7},{1,0},{2,1},{3,2},{4,3},{5,4},{6,5},{7,6},{8,15},{9,8},{10,9... | collective-permute-start | bytes 393224 | tf_op jit(solution)/shard_map/while/body/eval_jaxpr/ppermute | solution.py:91
  1027.1 24.4 %collective-permute-start.1 = (bf16[64,1024]{1,0:T(8,128)(2,1)S(1)}, bf16[64,1024]{1,0:T(8,128)(2,1)S(1)}, u32[]{:S(2)}, u32[]{:S(2)}) collective-permute-start(bf16[64,1024]{1,0:T(8,128)(2,1)S(1)} %get-tuple-element.707), channel_id=1, source_target_pairs={{0,7},{1,0},{2,1},{3,2},{4,3},{5,4},{6,5},{7,6},{8,15},{9,8},{10,9... | collective-permute-start | bytes 393224 | tf_op jit(solution)/shard_map/while/body/eval_jaxpr/ppermute | solution.py:91
  1053.9 593.5 %all-reduce.3.cloned.1.call-start = ((), (), s32[]{:S(2)}) async-start(), calls=%async_computation.6 | async-start | bytes 67108864 | tf_op jit(solution)/shard_map/psum | solution.py:101
  1647.4 16.4 copy-start.1
  (63 other events, 600.3 us)
Sparse Core Ops, SparseCore 0:
  9.6 23.0 all-gather.2
  34.4 20.3 all-gather.4
  399.2 28.8 reduce-scatter.2
  1054.0 31.3 reduce-scatter.4
  1088.5 558.8 all-reduce.2
where the time goes:
time: 1680 us
  waiting for transfers between devices  702 us (42%)
  matrix products  667 us (40%)
  other arithmetic  184 us (11%)
  local copies, waits for them, and re-layouts  60.8 us (4%)
  loops' own time  41.6 us (2%)
    psum x1, waiting for transfers between devices, body(): dw1 = lax.psum(dw1, 'inner')  562 us
    dot_general x15, matrix products, _bwd(): dw2 = jnp.dot(a.T, dh, preferred_element_type=jnp.float32)  172 us
    dot_general x15, matrix products, _bwd(): dw1 = jnp.dot(h.T, dz, preferred_element_type=jnp.float32)  170 us
    dot_general x15, matrix products, _fwd(): u = jnp.dot(a, w2, preferred_element_type=jnp.float32)  146 us
    another operation x60, other arithmetic  86.8 us
    ppermute x15, waiting for transfers between devices, fwd_tick(): inc = lax.ppermute(h, 'stage', fwd_perm)  83.4 us
    dot_general x15, matrix products, _bwd(): z = jnp.dot(h, w1, preferred_element_type=jnp.float32)  76.5 us
    dot_general x15, matrix products, _bwd(): jnp.dot(dz, w1.T, preferred_element_type=jnp.float32)  59.2 us
  transfers between devices with their start and end apart: 35, of which 18 were waited for; matrix products, arithmetic and copies ran while one was open for 53% of the time, Pallas kernels for 0%

commit v1 on v0

v1 whole, which is shorter than its diff:
```python
import functools

import jax
import jax.numpy as jnp
from jax import lax
from jax.experimental import pallas as pl
from jax.experimental.pallas import tpu as pltpu
from jax.sharding import PartitionSpec as P

MESH = pl.DeviceIdType.MESH
F32, BF16 = jnp.float32, jnp.bfloat16
C0, C1 = 0.7978845608028654, 0.044715
VMEM_LIMIT = 62 * 2**20


def _gelu(z):
    return z * (0.5 * (1.0 + jnp.tanh(C0 * (z + C1 * (z * z * z)))))


def _gelu_and_slope(z):
    z2 = z * z
    t = jnp.tanh(C0 * (z + C1 * (z2 * z)))
    half = 0.5 * (1.0 + t)
    return z * half, half + (0.5 * z) * (1.0 - t * t) * (C0 + (3.0 * C0 * C1) * z2)


def _dot(a, b):
    return jnp.dot(a, b, preferred_element_type=F32)


def _chain_kernel(
    n_stage, n_inner, x, g, w1, w2, y, dx, h_all, g_all,
    w1v, w2v, w1t, w2t, hs, gs, ho, go, zb, ab,
    wsem, xsem, h_recv, g_recv, h_send, g_send, out_recv, ring_send, ring_recv,
):
    p, i = lax.axis_index("stage"), lax.axis_index("inner")
    right, left = lax.rem(i + 1, n_inner), lax.rem(i + n_inner - 1, n_inner)
    m_all, rows, d = hs.shape
    f = w1v.shape[1]
    half = rows // 2
    last = n_stage - 1
    cw = min(512, f)

    loads = [
        pltpu.make_async_copy(w1.at[0, 0], w1v, wsem.at[0]),
        pltpu.make_async_copy(w2.at[0, 0], w2v, wsem.at[1]),
    ]
    for c in loads:
        c.start()

    barrier = pltpu.get_barrier_semaphore()
    for q in range(1, n_stage):
        pl.semaphore_signal(barrier, inc=1, device_id={"stage": lax.rem(p + q, n_stage)}, device_id_type=MESH)
    for q in (left, right):
        pl.semaphore_signal(barrier, inc=1, device_id={"inner": q}, device_id_type=MESH)
    pl.semaphore_wait(barrier, n_stage + 1)

    def to_stage(src, dst, send, recv, stage):
        return pltpu.make_async_remote_copy(
            src_ref=src, dst_ref=dst, send_sem=send, recv_sem=recv,
            device_id={"stage": stage}, device_id_type=MESH,
        )

    def to_inner(src, dst, send, recv, inner):
        return pltpu.make_async_remote_copy(
            src_ref=src, dst_ref=dst, send_sem=send, recv_sem=recv,
            device_id={"inner": inner}, device_id_type=MESH,
        )

    def own(src, slots, recv, sem, stage):
        @pl.when(p == stage)
        def _():
            pltpu.make_async_copy(src.at[0], slots.at[p], recv.at[p]).start()

        @pl.when(p != stage)
        def _():
            to_stage(src.at[0], slots.at[p], sem, recv.at[p], stage).start()

    own(x, hs, h_recv, xsem.at[0], 0)
    own(g, gs, g_recv, xsem.at[1], last)

    def ring_first(q, m, slots, whole):
        pltpu.make_async_copy(slots.at[m], whole.at[i, m], ring_send.at[q, m, 4]).start()
        to_inner(slots.at[m], whole.at[i, m], ring_send.at[q, m, 0], ring_recv.at[q, m, 0], right).start()
        to_inner(slots.at[m], whole.at[i, m], ring_send.at[q, m, 1], ring_recv.at[q, m, 1], left).start()

    def ring_forward(q, m, whole):
        a, b = whole.at[left, m], whole.at[right, m]
        to_inner(a, a, ring_send.at[q, m, 0], ring_recv.at[q, m, 0], right).wait_recv()
        a = whole.at[left, m, pl.ds(0, half)]
        to_inner(a, a, ring_send.at[q, m, 2], ring_recv.at[q, m, 2], right).start()
        to_inner(b, b, ring_send.at[q, m, 1], ring_recv.at[q, m, 1], left).wait_recv()
        b = whole.at[right, m, pl.ds(half, half)]
        to_inner(b, b, ring_send.at[q, m, 3], ring_recv.at[q, m, 3], left).start()

    def ring_finish(q, m, slots, whole):
        far = lax.rem(i + 2, n_inner)
        a, b = whole.at[far, m, pl.ds(0, half)], whole.at[far, m, pl.ds(half, half)]
        to_inner(a, a, ring_send.at[q, m, 2], ring_recv.at[q, m, 2], right).wait()
        to_inner(b, b, ring_send.at[q, m, 3], ring_recv.at[q, m, 3], left).wait()
        to_inner(slots.at[m], whole.at[i, m], ring_send.at[q, m, 0], ring_recv.at[q, m, 0], right).wait_send()
        to_inner(slots.at[m], whole.at[i, m], ring_send.at[q, m, 1], ring_recv.at[q, m, 1], left).wait_send()
        pltpu.make_async_copy(slots.at[m], whole.at[i, m], ring_send.at[q, m, 4]).wait()

    def pass_on(m, src, slots, send, recv, end, nxt, out, out_sem):
        @pl.when(p != end)
        def _():
            to_stage(src.at[m], slots.at[m], send.at[m], recv.at[m], nxt).start()

        @pl.when((p == end) & (p != m))
        def _():
            to_stage(src.at[m], out.at[0], send.at[m], out_sem, m).start()

        @pl.when((p == end) & (p == m))
        def _():
            pltpu.make_async_copy(src.at[m], out.at[0], out_sem).start()

    def forward(m):
        pltpu.make_async_copy(hs.at[m], hs.at[m], h_recv.at[m]).wait()
        ring_first(0, m, hs, h_all)
        h = hs[m]
        for c in range(0, f, cw):
            z = _dot(h, w1v[:, c : c + cw])
            zb[m, :, c : c + cw] = z
            ab[:, c : c + cw] = _gelu(z).astype(BF16)
        ho[m] = (h.astype(F32) + _dot(ab[...], w2v[...])).astype(BF16)
        pass_on(m, ho, hs, h_send, h_recv, last, jnp.minimum(p + 1, last), y, out_recv.at[0])

    def backward(m):
        pltpu.make_async_copy(gs.at[m], gs.at[m], g_recv.at[m]).wait()
        ring_first(1, m, gs, g_all)

        @pl.when(p < n_stage - 2)
        def _():
            ring_forward(0, m, h_all)

        dh = gs[m]
        for c in range(0, f, cw):
            da = _dot(dh, w2t[:, c : c + cw])
            _, slope = _gelu_and_slope(zb[m, :, c : c + cw])
            ab[:, c : c + cw] = (da * slope).astype(BF16)
        go[m] = (dh.astype(F32) + _dot(ab[...], w1t[...])).astype(BF16)
        pass_on(m, go, gs, g_send, g_recv, 0, jnp.maximum(p - 1, 0), dx, out_recv.at[1])

    def transpose_weights():
        tw = min(256, d)

        def some(t, carry):
            s = pl.ds(pl.multiple_of(t * tw, tw), tw)
            w1t[s, :] = w1v[:, s].T
            w2t[:, s] = w2v[s, :].T
            return carry

        lax.fori_loop(0, f // tw, some, 0)

    for c in loads:
        c.wait()

    first = jnp.where(p == last, 1, jnp.where(p == last - 1, min(4, m_all), m_all))
    rest = m_all - first
    turn = jnp.where(p < n_stage // 2, first, 0)

    def step(k, carry):
        j = k - first
        alternating = j < 2 * rest
        is_f = (j < 0) | (alternating & (j % 2 == 1))
        m_f = jnp.where(j < 0, k, jnp.minimum(first + j // 2, m_all - 1))
        m_b = jnp.where(j < 0, 0, jnp.where(alternating, j // 2, j - rest))

        @pl.when(k == turn)
        def _():
            transpose_weights()

        @pl.when(is_f)
        def _():
            forward(m_f)

        @pl.when(jnp.logical_not(is_f))
        def _():
            backward(m_b)

        return carry

    lax.fori_loop(0, 2 * m_all, step, 0)

    def each(fn):
        lax.fori_loop(0, m_all, lambda m, c: (fn(m), c)[1], 0)

    @pl.when(p >= n_stage - 2)
    def _():
        each(lambda m: ring_forward(0, m, h_all))

    each(lambda m: ring_forward(1, m, g_all))

    def finish(m):
        ring_finish(0, m, hs, h_all)
        ring_finish(1, m, gs, g_all)

        @pl.when((p != last) | (p != m))
        def _():
            to_stage(ho.at[m], hs.at[m], h_send.at[m], h_recv.at[m], 0).wait_send()

        @pl.when((p != 0) | (p != m))
        def _():
            to_stage(go.at[m], gs.at[m], g_send.at[m], g_recv.at[m], 0).wait_send()

    each(finish)

    @pl.when(p != 0)
    def _():
        to_stage(x.at[0], hs.at[0], xsem.at[0], h_recv.at[0], 0).wait_send()

    @pl.when(p != last)
    def _():
        to_stage(g.at[0], gs.at[0], xsem.at[1], g_recv.at[0], last).wait_send()

    pltpu.make_async_copy(y.at[0], y.at[0], out_recv.at[0]).wait()
    pltpu.make_async_copy(dx.at[0], dx.at[0], out_recv.at[1]).wait()


def _chain(n_stage, n_inner, x, g, w1, w2):
    mb, rows, d = x.shape
    f = w1.shape[-1]
    m_all = mb * n_stage
    hbm = pl.BlockSpec(memory_space=pltpu.HBM)
    whole = jax.ShapeDtypeStruct((n_inner, m_all, rows, d), BF16)
    dma = pltpu.SemaphoreType.DMA
    slots = pltpu.VMEM((m_all, rows, d), BF16)
    return pl.pallas_call(
        functools.partial(_chain_kernel, n_stage, n_inner),
        out_shape=[jax.ShapeDtypeStruct(x.shape, BF16), jax.ShapeDtypeStruct(x.shape, BF16), whole, whole],
        in_specs=[hbm] * 4,
        out_specs=[hbm] * 4,
        scratch_shapes=[
            pltpu.VMEM((d, f), BF16), pltpu.VMEM((f, d), BF16),
            pltpu.VMEM((f, d), BF16), pltpu.VMEM((d, f), BF16),
            slots, slots, slots, slots,
            pltpu.VMEM((m_all, rows, f), F32), pltpu.VMEM((rows, f), BF16),
            dma((2,)), dma((2,)), dma((m_all,)), dma((m_all,)), dma((m_all,)), dma((m_all,)), dma((2,)),
            dma((2, m_all, 5)), dma((2, m_all, 4)),
        ],
        compiler_params=pltpu.CompilerParams(
            collective_id=0, has_side_effects=True, vmem_limit_bytes=VMEM_LIMIT
        ),
        name="chain",
    )(x, g, w1, w2)


def _dw_kernel(tc, h, g, w1, w2, d1, d2, ht, ab, zb):
    t_all, _ = h.shape

    @pl.when(pl.program_id(0) == 0)
    def _():
        tw = min(256, t_all)
        for t in range(0, t_all, tw):
            ht[:, t : t + tw] = h[t : t + tw, :].T

    def some(t, carry):
        s = pl.ds(pl.multiple_of(t * tc, tc), tc)
        z = _dot(h[s, :], w1[...])
        da = lax.dot_general(g[s, :], w2[...], (((1,), (1,)), ((), ())), preferred_element_type=F32)
        a, slope = _gelu_and_slope(z)
        ab[s, :] = a.astype(BF16)
        zb[s, :] = (da * slope).astype(BF16)
        return carry

    lax.fori_loop(0, t_all // tc, some, 0)
    d1[...] = _dot(ht[...], zb[...])
    d2[...] = lax.dot_general(ab[...], g[...], (((0,), (0,)), ((), ())), preferred_element_type=F32)


def _dw(h, g, w1, w2):
    t, d = h.shape
    f = w1.shape[1]
    blk = min(512, f)
    return pl.pallas_call(
        functools.partial(_dw_kernel, min(512, t)),
        grid=(f // blk,),
        in_specs=[
            pl.BlockSpec((t, d), lambda j: (0, 0)), pl.BlockSpec((t, d), lambda j: (0, 0)),
            pl.BlockSpec((d, blk), lambda j: (0, j)), pl.BlockSpec((blk, d), lambda j: (j, 0)),
        ],
        out_specs=[pl.BlockSpec((d, blk), lambda j: (0, j)), pl.BlockSpec((blk, d), lambda j: (j, 0))],
        out_shape=[jax.ShapeDtypeStruct((d, f), F32), jax.ShapeDtypeStruct((f, d), F32)],
        scratch_shapes=[pltpu.VMEM((d, t), BF16), pltpu.VMEM((t, blk), BF16), pltpu.VMEM((t, blk), BF16)],
        compiler_params=pltpu.CompilerParams(vmem_limit_bytes=VMEM_LIMIT),
        cost_estimate=pl.CostEstimate(flops=8 * t * d * f, bytes_accessed=12 * d * f, transcendentals=t * f),
        name="dw",
    )(h, g, w1, w2)


def solution(mesh):
    n_stage, n_inner = mesh.shape["stage"], mesh.shape["inner"]

    def body(x, g, w1, w2):
        d, f = w1.shape[-2:]
        y, dx, h_all, g_all = _chain(n_stage, n_inner, x, g, w1, w2)
        d1, d2 = _dw(h_all.reshape(-1, d), g_all.reshape(-1, d), w1.reshape(d, f), w2.reshape(f, d))
        return y, dx, d1.reshape(w1.shape), d2.reshape(w2.shape)

    tok = P(("data", "stage"), "inner", None)
    wsp = P(None, "stage", None, None)
    dsp = P("data", "stage", None, None)
    return jax.shard_map(body, mesh=mesh, in_specs=(tok, tok, wsp, wsp), out_specs=(tok, tok, dsp, dsp), check_vma=False)
```

time: 1680 us -> 235 us (0.14)
  waiting for transfers between devices: 702 us -> 0 us
  matrix products: 667 us -> 0 us
  Pallas kernels: 0 us -> 233 us
  other arithmetic: 184 us -> 0 us
  local copies, waits for them, and re-layouts: 60.8 us -> 1.32 us
  loops' own time: 41.6 us -> 0 us
    dot_general x90 -> x0, matrix products: 667 us -> none  [the longest x15 172 us: _bwd(): dw2 = jnp.dot(a.T, dh, preferred_element_type=jnp.float32)]
    psum x1 -> x0, waiting for transfers between devices: 562 us -> none  [body(): dw1 = lax.psum(dw1, 'inner')]
    pallas_call x0 -> x2, Pallas kernels: none -> 233 us  [the longest x1 147 us: _chain(): pl.pallas_call(functools.partial(_chain_kernel, n_stage, n_inner), out_sh...]
    another operation x60 -> x0, other arithmetic: 86.8 us -> none
    ppermute x30 -> x0, waiting for transfers between devices: 83.4 us -> none  [the longest x15 83.4 us: fwd_tick(): inc = lax.ppermute(h, 'stage', fwd_perm)]
    scatter x45 -> x0, other arithmetic: 78.5 us -> none  [the longest x15 32.4 us: bwd_tick(): buf = buf.at[m_in].set(jnp.where(ok_in & (q == 0), inc, buf[m_in]))]
    another operation x2 -> x0, loops' own time: 41.6 us -> none  [the longest x1 21.6 us: body(): lax.scan(bwd_tick, (act0, per_mb0, dw1_0, dw2_0, per_mb0), ticks)]
    dynamic_slice x75 -> x0, local copies, waits for them, and re-layouts: 33.9 us -> none  [the longest x30 19.7 us: body(): lax.scan(fwd_tick, (act0, per_mb0, saved0, per_mb0), ticks)]
  transfers between devices with their start and end apart: 35 -> 0, of which waited for: 18 -> 0; matrix products, arithmetic and copies ran while one was open for 53% -> 0% of each run, Pallas kernels for 0% -> 0%
where the time goes in v1:
time: 235 us
  Pallas kernels  233 us (99%)
    pallas_call x1, Pallas kernels, _chain(): pl.pallas_call(functools.partial(_chain_kernel, n_stage, n_inner), out_sh...  147 us
    pallas_call x1, Pallas kernels, _dw(): pl.pallas_call(functools.partial(_dw_kernel, min(512, t)), grid=(f // blk...  86.7 us

profile of v1, /device:TPU:96, one launch (start us, length us, event | category | flops | bytes accessed | tf_op | source)
XLA Modules:
  0.0 235.3 jit_solution(9981249127386753030)
XLA Ops:
  0.6 146.7 %chain.1 = (bf16[1,64,1024]{2,1,0:T(8,128)(2,1)}, bf16[1,64,1024]{2,1,0:T(8,128)(2,1)}, bf16[4,8,64,1024]{3,2,1,0:T(8,128)(2,1)}, bf16[4,8,64,1024]{3,2,1,0:T(8,128)(2,1)}) custom-call(bf16[1,64,1024]{2,1,0:T(8,128)(2,1)} %x.1, bf16[1,64,1024]{2,1,0:T(8,128)(2,1)} %g.1, bf16[1,1,1024,4096]{3,2,1,0:T(8,128)(2,1)} %w1.1, bf16[1,1,4096,1024]{3,2,1,0:T(8,128)(2,1)} %w2.1), custom_call_target="tpu_custom_call" | custom-call | tf_op jit(solution)/shard_map/chain/pallas_call | solution.py:229
  147.3 0.0 copy-start.1
  147.3 0.0 copy-start
  147.3 86.7 %dw.1 = (f32[1024,4096]{1,0:T(8,128)}, f32[4096,1024]{1,0:T(8,128)}) custom-call(bf16[2048,1024]{1,0:T(8,128)(2,1)} %bitcast.8, bf16[2048,1024]{1,0:T(8,128)(2,1)} %bitcast.9, bf16[1024,4096]{1,0:T(8,128)(2,1)} %bitcast.6, bf16[4096,1024]{1,0:T(8,128)(2,1)} %bitcast.7), custom_call_target="tpu_custom_call" | custom-call | flops 68719476736 | bytes 50331648 | tf_op jit(solution)/shard_map/dw/pallas_call | solution.py:276
  234.0 0.0 copy-done.1
  234.0 0.7 copy.10
  234.7 0.0 copy-done
  234.7 0.7 copy.11
Async XLA Ops:
  147.3 86.7 %copy-start.1 = (bf16[1,64,1024]{2,1,0:T(8,128)(2,1)S(1)}, bf16[1,64,1024]{2,1,0:T(8,128)(2,1)}, u32[]{:S(2)}) copy-start(bf16[1,64,1024]{2,1,0:T(8,128)(2,1)} %get-tuple-element.20) | copy-start | bytes 393220
  147.3 87.4 %copy-start = (bf16[1,64,1024]{2,1,0:T(8,128)(2,1)S(1)}, bf16[1,64,1024]{2,1,0:T(8,128)(2,1)}, u32[]{:S(2)}) copy-start(bf16[1,64,1024]{2,1,0:T(8,128)(2,1)} %get-tuple-element.21) | copy-start | bytes 393220
